TPU v7x, 128 devices: a whole 4x4x4 slice. The times are simulated.
128 devices in a mesh: gx: 4 (over z_hi, core), gy: 4 (over x), gz: 8 (over y, z_lo).
Axes of the slice: x: 4, y: 4, z: 4 (z_hi: 2, z_lo: 2; z = z_hi * 2 + z_lo), core: 2. Of those that a mesh axis runs over, the one named last changes fastest.
Arguments:
- x_a: bfloat16 [32, 8, 64, 1024], P(None, 'gx', 'gy', 'gz'), may hold values from -12 to 12
- x_b: bfloat16 [32, 8, 64, 1024], P(None, 'gx', 'gy', 'gz'), may hold values from -12 to 12
- w_first: bfloat16 [3, 3, 3, 32, 32], replicated, may hold values from -0.21875 to 0.21875
- w_second: bfloat16 [3, 3, 3, 32, 32], replicated, may hold values from -0.21875 to 0.21875
- gain_first: float32 [32], replicated, may hold values from 0.1 to 1.9
- bias_first: float32 [32], replicated, may hold values from -2 to 2
- gain_second: float32 [32], replicated, may hold values from 0.1 to 1.9
- bias_second: float32 [32], replicated, may hold values from -2 to 2
- grad_out: bfloat16 [32, 8, 64, 1024], P(None, 'gx', 'gy', 'gz'), may hold values from -6 to 6
Outputs:
- y_a: bfloat16 [32, 8, 64, 1024], P(None, 'gx', 'gy', 'gz')
- dx_b: bfloat16 [32, 8, 64, 1024], P(None, 'gx', 'gy', 'gz')
- grad_w_first: float32 [3, 3, 3, 32, 32], replicated
- grad_w_second: float32 [3, 3, 3, 32, 32], replicated
- grad_norm: float32 [4, 32], replicated
All inputs are finite; a program needn't handle non-finite values.
Results may differ from a plain program's by a relative error of at most 0.0063.
Values may be sent and summed in bfloat16 or wider, within the bound.
A program may use at most 128 MiB of HBM per device.

v0:
```python
import functools
import math
import jax
import jax.numpy as jnp
from jax import lax
from jax.sharding import Mesh
from jax.sharding import PartitionSpec as P

GX_GY_GZ = ("gx_0", "gx_1", "gy", "gz_0", "gz_1")
GX = ("gx_0", "gx_1")
GZ = ("gz_0", "gz_1")
EPSILON = 1e-05


def by_axis(value, axes):
    return functools.reduce(lax.psum, axes, value)


def extended(block, sides, width):
    for axis, dim in sides:
        count = lax.axis_size(axis)
        forward = [(i, i + 1) for i in range(count - 1)]
        backward = [(target, source) for source, target in forward]
        low = lax.ppermute(
            lax.slice_in_dim(block, block.shape[dim] - width, None, axis=dim), axis, forward
        )
        high = lax.ppermute(lax.slice_in_dim(block, 0, width, axis=dim), axis, backward)
        block = jnp.concatenate([low, block, high], axis=dim)
    return block


def spread(values):
    return values[:, None, None, None]


def silu_slope(value):
    sigma = jax.nn.sigmoid(value)
    return sigma * (1.0 + value * (1.0 - sigma))


def convolve(padded, weight):
    in_chan = padded.shape[0]
    out_chan = weight.shape[3]
    span_x = padded.shape[1] - 2
    span_y = padded.shape[2] - 2
    span_z = padded.shape[3] - 2
    total = jnp.zeros((out_chan, span_x * span_y * span_z), jnp.float32)
    for shift_x in range(3):
        for shift_y in range(3):
            pieces = [
                padded[
                    :,
                    shift_x : shift_x + span_x,
                    shift_y : shift_y + span_y,
                    shift_z : shift_z + span_z,
                ]
                for shift_z in range(3)
            ]
            stacked = jnp.concatenate(pieces, axis=0).reshape(3 * in_chan, -1)
            matrix = weight[shift_x, shift_y].transpose(1, 0, 2).reshape(out_chan, 3 * in_chan)
            total = total + jnp.dot(matrix, stacked, preferred_element_type=jnp.float32)
    return total.reshape(out_chan, span_x, span_y, span_z)


def kernel_grad(padded, upstream):
    in_chan = padded.shape[0]
    out_chan = upstream.shape[0]
    span_x, span_y, span_z = (upstream.shape[1], upstream.shape[2], upstream.shape[3])
    flat = upstream.reshape(out_chan, -1)
    rows = []
    for shift_x in range(3):
        for shift_y in range(3):
            pieces = [
                padded[
                    :,
                    shift_x : shift_x + span_x,
                    shift_y : shift_y + span_y,
                    shift_z : shift_z + span_z,
                ]
                for shift_z in range(3)
            ]
            stacked = jnp.concatenate(pieces, axis=0).reshape(3 * in_chan, -1)
            product = lax.dot_general(
                flat, stacked, (((1,), (1,)), ((), ())), preferred_element_type=jnp.float32
            )
            rows.append(product.reshape(out_chan, 3, in_chan).transpose(1, 0, 2))
    return jnp.stack(rows).reshape(3, 3, 3, out_chan, in_chan)


def flipped(weight):
    return jnp.flip(weight, (0, 1, 2)).transpose(0, 1, 2, 4, 3)


def statistics(blocks, voxels):
    local_sums = jnp.stack([jnp.sum(block, axis=(1, 2, 3)) for block in blocks])
    local_squares = jnp.stack([jnp.sum(jnp.square(block), axis=(1, 2, 3)) for block in blocks])
    sums, squares = (by_axis(local_sums, GX_GY_GZ), by_axis(local_squares, GX_GY_GZ))
    means = sums / voxels
    variance = squares / voxels - means * means
    return (means, lax.rsqrt(variance + EPSILON))


def normalize(block, means, scales, gain, bias):
    normed = (block - spread(means)) * spread(scales)
    return (normed, spread(gain) * normed + spread(bias))


def backward_layer(upstream, preact, normed, scales, gain, voxels):
    slope = upstream * silu_slope(preact)
    sum_d, sum_dx = (
        by_axis(jnp.sum(slope, axis=(1, 2, 3)), GX_GY_GZ),
        by_axis(jnp.sum(slope * normed, axis=(1, 2, 3)), GX_GY_GZ),
    )
    delta = spread(gain * scales) * (
        slope - spread(sum_d / voxels) - normed * spread(sum_dx / voxels)
    )
    return (delta.astype(jnp.bfloat16), sum_d, sum_dx)


def body(x_a, x_b, w_first, w_second, gain_first, bias_first, gain_second, bias_second, grad_out):
    rows_x, rows_y, rows_z = (x_a.shape[1], x_a.shape[2], x_a.shape[3])
    voxels = float(
        rows_x * rows_y * rows_z * lax.axis_size(GX) * lax.axis_size("gy") * lax.axis_size(GZ)
    )
    factor = 1.0 / math.sqrt(voxels)
    volumes = jnp.stack([x_a, x_b])
    padded = extended(volumes, ((GX, 2), ("gy", 3), (GZ, 4)), 1)
    first = [convolve(padded[member], w_first) for member in range(2)]
    means, scales = statistics(first, voxels)
    hidden = []
    for member in range(2):
        normed, preact = normalize(
            first[member], means[member], scales[member], gain_first, bias_first
        )
        hidden.append((preact * jax.nn.sigmoid(preact)).astype(jnp.bfloat16))
    hidden_all = extended(jnp.stack(hidden), ((GX, 2), ("gy", 3), (GZ, 4)), 1)
    hidden_pads = [hidden_all[0], hidden_all[1]]
    input_pad_b = padded[1]
    scale_one = scales[1]
    second = [convolve(hidden_pads[member], w_second) for member in range(2)]
    means_two, scales_two = statistics(second, voxels)
    normed_a, preact_a = normalize(second[0], means_two[0], scales_two[0], gain_second, bias_second)
    y_a = (preact_a * jax.nn.sigmoid(preact_a)).astype(jnp.bfloat16)
    norm_two, pre_two = normalize(second[1], means_two[1], scales_two[1], gain_second, bias_second)
    delta_two, sum_d2, sum_x2 = backward_layer(
        grad_out.astype(jnp.float32), pre_two, norm_two, scales_two[1], gain_second, voxels
    )
    local_second = kernel_grad(hidden_pads[1], delta_two) * factor
    grad_w_second = lax.psum(local_second, GX_GY_GZ)
    delta_pad_two = extended(delta_two, ((GX, 1), ("gy", 2), (GZ, 3)), 1)
    upstream_one = convolve(delta_pad_two, flipped(w_second))
    delta_one, sum_d1, sum_x1 = backward_layer(
        upstream_one, preact, normed, scale_one, gain_first, voxels
    )
    local_first = kernel_grad(input_pad_b, delta_one) * factor
    delta_pad_one = extended(delta_one, ((GX, 1), ("gy", 2), (GZ, 3)), 1)
    dx_b = convolve(delta_pad_one, flipped(w_first)).astype(jnp.bfloat16)
    grad_w_first = lax.psum(local_first, GX_GY_GZ)
    grad_norm = jnp.stack([sum_x1, sum_d1, sum_x2, sum_d2]) * factor
    return (y_a, dx_b, grad_w_first, grad_w_second, grad_norm)


def solution(mesh):
    torus = Mesh(
        mesh.devices.reshape(2, 2, mesh.shape["gy"], 4, 2), ("gx_0", "gx_1", "gy", "gz_0", "gz_1")
    )
    in_specs = (
        P(None, GX, "gy", GZ),
        P(None, GX, "gy", GZ),
        P(),
        P(),
        P(),
        P(),
        P(),
        P(),
        P(None, GX, "gy", GZ),
    )
    out_specs = (P(None, GX, "gy", GZ), P(None, GX, "gy", GZ), P(), P(), P())
    return jax.shard_map(body, mesh=torus, in_specs=in_specs, out_specs=out_specs, check_vma=False)
```

profile of v0, /device:TPU:1, one launch (start us, length us, event | category | flops | bytes accessed | tf_op | source)
XLA Modules:
  0.0 573.7 jit_solution(8080305644700961799)
XLA Ops:
  8.4 6.9 %collective-permute-start = (bf16[2,32,1,16,128]{4,3,2,1,0:T(8,128)(2,1)S(1)}, bf16[2,32,1,16,128]{4,3,2,1,0:T(8,128)(2,1)S(1)}, u32[]{:S(2)}, u32[]{:S(2)}) collective-permute-start(bf16[2,32,1,16,128]{4,3,2,1,0:T(8,128)(2,1)S(1)} %get-tuple-element.259), channel_id=1, source_target_pairs={{0,32},{32,64},{64,96},{1,33},{33,65},{65,97},{2,34},{34,66},{66,9... | collective-permute-start | bytes 786440 | tf_op jit(solution)/shard_map/ppermute | solution.py:24
  18.6 5.9 %collective-permute-done.1 = bf16[2,32,1,16,128]{4,3,2,1,0:T(8,128)(2,1)S(1)} collective-permute-done((bf16[2,32,1,16,128]{4,3,2,1,0:T(8,128)(2,1)S(1)}, bf16[2,32,1,16,128]{4,3,2,1,0:T(8,128)(2,1)S(1)}, u32[]{:S(2)}, u32[]{:S(2)}) %collective-permute-start.1) | collective-permute-done | bytes 262176 | tf_op jit(solution)/shard_map/ppermute | solution.py:27
  36.1 3.8 collective-permute-done.3
  39.9 6.2 %pad_maximum_fusion = bf16[2,32,4,18,128]{1,2,4,3,0:T(4,128)(2,1)S(1)} fusion(bf16[2,32,4,1,128]{1,2,4,3,0:T(4,128)(2,1)S(1)} %collective-permute-done.3, bf16[2,32,4,16,128]{1,2,4,3,0:T(4,128)(2,1)} %copy.460, bf16[2,32,4,1,128]{1,2,4,3,0:T(4,128)(2,1)S(1)} %collective-permute-done.2), kind=kLoop, calls=%fused_computation | loop fusion | flops 1179648 | bytes 2359296 | tf_op jit(solution)/shard_map/concatenate | solution.py:28
  58.7 6.3 %copy.464 = bf16[2,32,4,18,128]{4,1,3,2,0:T(8,128)(2,1)S(1)} copy(bf16[2,32,4,18,128]{1,2,4,3,0:T(4,128)(2,1)} %copy-done) | data formatting | bytes 2359296 | tf_op jit(solution)/shard_map/concatenate | solution.py:28
  99.3 5.3 all-reduce.20
  107.0 7.2 %all-reduce.8 = (f32[2,32]{1,0:T(2,128)S(1)}, f32[2,32]{1,0:T(2,128)S(1)}) all-reduce(f32[2,32]{1,0:T(2,128)S(1)} %get-tuple-element.61, f32[2,32]{1,0:T(2,128)S(1)} %get-tuple-element.62), channel_id=1, replica_groups=mesh['gx_0'=2,'gx_1'=2,'gy'=4,'gz_0'=4,'gz_1'=2] {'gy'}, use_global_device_ids=true, to_apply=%region_11.0 | all-reduce | flops 128 | bytes 1024 | tf_op jit(solution)/shard_map/psum | solution.py:16
  114.2 10.4 %all-reduce.4 = (f32[2,32]{1,0:T(2,128)S(1)}, f32[2,32]{1,0:T(2,128)S(1)}) all-reduce(f32[2,32]{1,0:T(2,128)S(1)} %get-tuple-element.45, f32[2,32]{1,0:T(2,128)S(1)} %get-tuple-element.46), channel_id=1, replica_groups=mesh['gx_0'=2,'gx_1'=2,'gy'=4,'gz_0'=4,'gz_1'=2] {'gz_0'}, use_global_device_ids=true, to_apply=%region_12.0 | all-reduce | flops 128 | bytes 1024 | tf_op jit(solution)/shard_map/psum | solution.py:16
  124.6 3.8 all-reduce.12
  130.7 10.1 %collective-permute-start.6 = (bf16[2,32,1,16,128]{4,3,2,1,0:T(8,128)(2,1)S(1)}, bf16[2,32,1,16,128]{4,3,2,1,0:T(8,128)(2,1)S(1)}, u32[]{:S(2)}, u32[]{:S(2)}) collective-permute-start(bf16[2,32,1,16,128]{4,3,2,1,0:T(8,128)(2,1)S(1)} %get-tuple-element.257), channel_id=1, source_target_pairs={{0,32},{32,64},{64,96},{1,33},{33,65},{65,97},{2,34},{34,66},{66,9... | collective-permute-start | bytes 786440 | tf_op jit(solution)/shard_map/ppermute | solution.py:24
  144.0 5.9 %collective-permute-done.7 = bf16[2,32,1,16,128]{4,3,2,1,0:T(8,128)(2,1)S(1)} collective-permute-done((bf16[2,32,1,16,128]{4,3,2,1,0:T(8,128)(2,1)S(1)}, bf16[2,32,1,16,128]{4,3,2,1,0:T(8,128)(2,1)S(1)}, u32[]{:S(2)}, u32[]{:S(2)}) %collective-permute-start.7) | collective-permute-done | bytes 262176 | tf_op jit(solution)/shard_map/ppermute | solution.py:27
  151.0 5.6 copy.493
  168.4 6.3 %pad_maximum_fusion.1 = bf16[2,32,4,18,128]{1,2,4,3,0:T(4,128)(2,1)S(1)} fusion(bf16[2,32,4,1,128]{1,2,4,3,0:T(4,128)(2,1)} %collective-permute-done.9, bf16[2,32,4,16,128]{1,2,4,3,0:T(4,128)(2,1)} %copy.493, bf16[2,32,4,1,128]{1,2,4,3,0:T(4,128)(2,1)S(1)} %collective-permute-done.8), kind=kLoop, calls=%fused_computation.1 | loop fusion | flops 1179648 | bytes 2359296 | tf_op jit(solution)/shard_map/concatenate | solution.py:28
  192.0 7.1 %copy.497 = bf16[2,32,4,18,128]{4,1,3,2,0:T(8,128)(2,1)} copy(bf16[2,32,4,18,128]{1,2,4,3,0:T(4,128)(2,1)} %copy-done.1) | data formatting | bytes 2359296 | tf_op jit(solution)/shard_map/concatenate | solution.py:28
  254.1 5.3 all-reduce.19
  261.9 8.3 %all-reduce.7 = (f32[2,32]{1,0:T(2,128)S(1)}, f32[2,32]{1,0:T(2,128)S(1)}) all-reduce(f32[2,32]{1,0:T(2,128)S(1)} %get-tuple-element.59, f32[2,32]{1,0:T(2,128)S(1)} %get-tuple-element.60), channel_id=1, replica_groups=mesh['gx_0'=2,'gx_1'=2,'gy'=4,'gz_0'=4,'gz_1'=2] {'gy'}, use_global_device_ids=true, to_apply=%region_25.0 | all-reduce | flops 128 | bytes 1024 | tf_op jit(solution)/shard_map/psum | solution.py:16
  270.2 8.6 %all-reduce.3 = (f32[2,32]{1,0:T(2,128)S(1)}, f32[2,32]{1,0:T(2,128)S(1)}) all-reduce(f32[2,32]{1,0:T(2,128)S(1)} %get-tuple-element.43, f32[2,32]{1,0:T(2,128)S(1)} %get-tuple-element.44), channel_id=1, replica_groups=mesh['gx_0'=2,'gx_1'=2,'gy'=4,'gz_0'=4,'gz_1'=2] {'gz_0'}, use_global_device_ids=true, to_apply=%region_26.0 | all-reduce | flops 128 | bytes 1024 | tf_op jit(solution)/shard_map/psum | solution.py:16
  278.8 3.8 all-reduce.11
  284.6 5.3 all-reduce.18
  289.9 8.6 %all-reduce.14 = (f32[32]{0:T(128)S(1)}, f32[32]{0:T(128)S(1)}) all-reduce(f32[32]{0:T(128)S(1)} %get-tuple-element.65, f32[32]{0:T(128)S(1)} %get-tuple-element.66), channel_id=1, replica_groups=mesh['gx_0'=2,'gx_1'=2,'gy'=4,'gz_0'=4,'gz_1'=2] {'gx_1'}, use_global_device_ids=true, to_apply=%region_36.0 | all-reduce | flops 64 | bytes 512 | tf_op jit(solution)/shard_map/psum | solution.py:16
  298.5 6.1 %all-reduce.6 = (f32[32]{0:T(128)S(1)}, f32[32]{0:T(128)S(1)}) all-reduce(f32[32]{0:T(128)S(1)} %get-tuple-element.57, f32[32]{0:T(128)S(1)} %get-tuple-element.58), channel_id=1, replica_groups=mesh['gx_0'=2,'gx_1'=2,'gy'=4,'gz_0'=4,'gz_1'=2] {'gy'}, use_global_device_ids=true, to_apply=%region_37.0 | all-reduce | flops 64 | bytes 512 | tf_op jit(solution)/shard_map/psum | solution.py:16
  304.6 6.2 %all-reduce.2 = (f32[32]{0:T(128)S(1)}, f32[32]{0:T(128)S(1)}) all-reduce(f32[32]{0:T(128)S(1)} %get-tuple-element.41, f32[32]{0:T(128)S(1)} %get-tuple-element.42), channel_id=1, replica_groups=mesh['gx_0'=2,'gx_1'=2,'gy'=4,'gz_0'=4,'gz_1'=2] {'gz_0'}, use_global_device_ids=true, to_apply=%region_38.0 | all-reduce | flops 64 | bytes 512 | tf_op jit(solution)/shard_map/psum | solution.py:16
  310.7 3.9 all-reduce.10
  318.2 9.4 %collective-permute-start.12 = (bf16[32,1,16,128]{3,0,2,1:T(8,128)(2,1)}, bf16[32,1,16,128]{3,0,2,1:T(8,128)(2,1)S(1)}, u32[]{:S(2)}, u32[]{:S(2)}) collective-permute-start(bf16[32,1,16,128]{3,0,2,1:T(8,128)(2,1)} %get-tuple-element.269), channel_id=1, source_target_pairs={{0,32},{32,64},{64,96},{1,33},{33,65},{65,97},{2,34},{34,66},{66,9... | collective-permute-start | bytes 393224 | tf_op jit(solution)/shard_map/ppermute | solution.py:24
  348.0 4.0 collective-permute-start.16
  366.1 5.4 all-reduce.17
  371.5 5.9 %all-reduce.13 = (f32[32]{0:T(128)S(1)}, f32[32]{0:T(128)S(1)}) all-reduce(f32[32]{0:T(128)S(1)} %get-tuple-element.63, f32[32]{0:T(128)S(1)} %get-tuple-element.64), channel_id=1, replica_groups=mesh['gx_0'=2,'gx_1'=2,'gy'=4,'gz_0'=4,'gz_1'=2] {'gx_1'}, use_global_device_ids=true, to_apply=%region_48.49 | all-reduce | flops 64 | bytes 512 | tf_op jit(solution)/shard_map/psum | solution.py:16
  377.4 6.1 %all-reduce.5 = (f32[32]{0:T(128)S(1)}, f32[32]{0:T(128)S(1)}) all-reduce(f32[32]{0:T(128)S(1)} %get-tuple-element.55, f32[32]{0:T(128)S(1)} %get-tuple-element.56), channel_id=1, replica_groups=mesh['gx_0'=2,'gx_1'=2,'gy'=4,'gz_0'=4,'gz_1'=2] {'gy'}, use_global_device_ids=true, to_apply=%region_49.50 | all-reduce | flops 64 | bytes 512 | tf_op jit(solution)/shard_map/psum | solution.py:16
  383.5 10.0 %all-reduce.1 = (f32[32]{0:T(128)S(1)}, f32[32]{0:T(128)S(1)}) all-reduce(f32[32]{0:T(128)S(1)} %get-tuple-element.39, f32[32]{0:T(128)S(1)} %get-tuple-element.40), channel_id=1, replica_groups=mesh['gx_0'=2,'gx_1'=2,'gy'=4,'gz_0'=4,'gz_1'=2] {'gz_0'}, use_global_device_ids=true, to_apply=%region_50.51 | all-reduce | flops 64 | bytes 512 | tf_op jit(solution)/shard_map/psum | solution.py:16
  398.3 10.4 %collective-permute-start.18 = (bf16[32,1,16,128]{3,0,2,1:T(8,128)(2,1)S(1)}, bf16[32,1,16,128]{3,0,2,1:T(8,128)(2,1)S(1)}, u32[]{:S(2)}, u32[]{:S(2)}) collective-permute-start(bf16[32,1,16,128]{3,0,2,1:T(8,128)(2,1)S(1)} %get-tuple-element.264), channel_id=1, source_target_pairs={{0,32},{32,64},{64,96},{1,33},{33,65},{65,97},{2,34},{34,66},{66,9... | collective-permute-start | bytes 393224 | tf_op jit(solution)/shard_map/ppermute | solution.py:24
  428.7 4.0 collective-permute-start.22
  444.8 118.3 %all-reduce.23.cloned.1.call-done = (f32[3,3,3,32,32]{4,3,2,1,0:T(8,128)}, f32[3,3,3,32,32]{4,3,2,1,0:T(8,128)}) async-done(((f32[3,3,3,32,32]{4,3,2,1,0:T(8,128)}, f32[3,3,3,32,32]{4,3,2,1,0:T(8,128)}), (f32[3,3,3,32,32]{4,3,2,1,0:T(8,128)}, f32[3,3,3,32,32]{4,3,2,1,0:T(8,128)})) %all-reduce.23.cloned.1.call-update) | async-done | bytes 221200 | tf_op jit(solution)/shard_map/psum | solution.py:158
  (671 shorter events, 236.2 us)
Async XLA Ops:
  7.2 555.8 %all-reduce.23.cloned.1.call-start = ((), (), s32[]{:S(2)}) async-start(), calls=%async_computation | async-start | bytes 1769472 | tf_op jit(solution)/shard_map/psum | solution.py:158
  8.4 10.2 %collective-permute-start = (bf16[2,32,1,16,128]{4,3,2,1,0:T(8,128)(2,1)S(1)}, bf16[2,32,1,16,128]{4,3,2,1,0:T(8,128)(2,1)S(1)}, u32[]{:S(2)}, u32[]{:S(2)}) collective-permute-start(bf16[2,32,1,16,128]{4,3,2,1,0:T(8,128)(2,1)S(1)} %get-tuple-element.259), channel_id=1, source_target_pairs={{0,32},{32,64},{64,96},{1,33},{33,65},{65,97},{2,34},{34,66},{66,9... | collective-permute-start | bytes 786440 | tf_op jit(solution)/shard_map/ppermute | solution.py:24
  15.3 9.2 %collective-permute-start.1 = (bf16[2,32,1,16,128]{4,3,2,1,0:T(8,128)(2,1)S(1)}, bf16[2,32,1,16,128]{4,3,2,1,0:T(8,128)(2,1)S(1)}, u32[]{:S(2)}, u32[]{:S(2)}) collective-permute-start(bf16[2,32,1,16,128]{4,3,2,1,0:T(8,128)(2,1)S(1)} %get-tuple-element.260), channel_id=1, source_target_pairs={{32,0},{64,32},{96,64},{33,1},{65,33},{97,65},{34,2},{66,34},{98,6... | collective-permute-start | bytes 786440 | tf_op jit(solution)/shard_map/ppermute | solution.py:27
  29.6 6.4 %collective-permute-start.2 = (bf16[2,32,4,1,128]{1,2,4,3,0:T(4,128)(2,1)S(1)}, bf16[2,32,4,1,128]{1,2,4,3,0:T(4,128)(2,1)S(1)}, u32[]{:S(2)}, u32[]{:S(2)}) collective-permute-start(bf16[2,32,4,1,128]{1,2,4,3,0:T(4,128)(2,1)S(1)} %get-tuple-element.79), channel_id=1, source_target_pairs={{0,8},{8,16},{16,24},{1,9},{9,17},{17,25},{2,10},{10,18},{18,26},{... | collective-permute-start | bytes 196616 | tf_op jit(solution)/shard_map/ppermute | solution.py:24
  32.8 7.1 %collective-permute-start.3 = (bf16[2,32,4,1,128]{1,2,4,3,0:T(4,128)(2,1)S(1)}, bf16[2,32,4,1,128]{1,2,4,3,0:T(4,128)(2,1)S(1)}, u32[]{:S(2)}, u32[]{:S(2)}) collective-permute-start(bf16[2,32,4,1,128]{1,2,4,3,0:T(4,128)(2,1)S(1)} %get-tuple-element.80), channel_id=1, source_target_pairs={{8,0},{16,8},{24,16},{9,1},{17,9},{25,17},{10,2},{18,10},{26,18},{... | collective-permute-start | bytes 196616 | tf_op jit(solution)/shard_map/ppermute | solution.py:27
  48.3 17.7 %collective-permute-start.4 = (bf16[2,32,4,18,1]{1,2,4,3,0:T(4,128)(2,1)S(1)}, bf16[2,32,4,18,1]{1,2,4,3,0:T(4,128)(2,1)}, u32[]{:S(2)}, u32[]{:S(2)}) collective-permute-start(bf16[2,32,4,18,1]{1,2,4,3,0:T(4,128)(2,1)S(1)} %get-tuple-element.75), channel_id=1, source_target_pairs={{0,1},{1,2},{2,3},{3,4},{4,5},{5,6},{6,7},{8,9},{9,10},{10,11},{11... | collective-permute-start | bytes 27656 | tf_op jit(solution)/shard_map/ppermute | solution.py:24
  51.5 13.5 %collective-permute-start.5 = (bf16[2,32,4,18,1]{1,2,4,3,0:T(4,128)(2,1)S(1)}, bf16[2,32,4,18,1]{1,2,4,3,0:T(4,128)(2,1)S(1)}, u32[]{:S(2)}, u32[]{:S(2)}) collective-permute-start(bf16[2,32,4,18,1]{1,2,4,3,0:T(4,128)(2,1)S(1)} %get-tuple-element.76), channel_id=1, source_target_pairs={{1,0},{2,1},{3,2},{4,3},{5,4},{6,5},{7,6},{9,8},{10,9},{11,10},{12... | collective-permute-start | bytes 27656 | tf_op jit(solution)/shard_map/ppermute | solution.py:27
  86.7 43.3 %copy-start.21 = (f32[4,8,32,128]{3,2,1,0:T(8,128)}, f32[4,8,32,128]{3,2,1,0:T(8,128)S(1)}, u32[]{:S(2)}) copy-start(f32[4,8,32,128]{3,2,1,0:T(8,128)S(1)} %copy.596) | copy-start | bytes 1572868
  96.7 33.4 %copy-start.147 = (f32[32]{0:T(128)S(1)}, f32[32]{0:T(128)}, u32[]{:S(2)}) copy-start(f32[32]{0:T(128)} %param.14) | copy-start | bytes 388
  96.8 33.4 %copy-start.149 = (f32[32]{0:T(128)S(1)}, f32[32]{0:T(128)}, u32[]{:S(2)}) copy-start(f32[32]{0:T(128)} %param.13) | copy-start | bytes 388
  130.7 13.4 %collective-permute-start.6 = (bf16[2,32,1,16,128]{4,3,2,1,0:T(8,128)(2,1)S(1)}, bf16[2,32,1,16,128]{4,3,2,1,0:T(8,128)(2,1)S(1)}, u32[]{:S(2)}, u32[]{:S(2)}) collective-permute-start(bf16[2,32,1,16,128]{4,3,2,1,0:T(8,128)(2,1)S(1)} %get-tuple-element.257), channel_id=1, source_target_pairs={{0,32},{32,64},{64,96},{1,33},{33,65},{65,97},{2,34},{34,66},{66,9... | collective-permute-start | bytes 786440 | tf_op jit(solution)/shard_map/ppermute | solution.py:24
  140.7 9.2 %collective-permute-start.7 = (bf16[2,32,1,16,128]{4,3,2,1,0:T(8,128)(2,1)S(1)}, bf16[2,32,1,16,128]{4,3,2,1,0:T(8,128)(2,1)S(1)}, u32[]{:S(2)}, u32[]{:S(2)}) collective-permute-start(bf16[2,32,1,16,128]{4,3,2,1,0:T(8,128)(2,1)S(1)} %get-tuple-element.258), channel_id=1, source_target_pairs={{32,0},{64,32},{96,64},{33,1},{65,33},{97,65},{34,2},{66,34},{98,6... | collective-permute-start | bytes 786440 | tf_op jit(solution)/shard_map/ppermute | solution.py:27
  158.7 9.2 %collective-permute-start.8 = (bf16[2,32,4,1,128]{1,2,4,3,0:T(4,128)(2,1)}, bf16[2,32,4,1,128]{1,2,4,3,0:T(4,128)(2,1)S(1)}, u32[]{:S(2)}, u32[]{:S(2)}) collective-permute-start(bf16[2,32,4,1,128]{1,2,4,3,0:T(4,128)(2,1)} %get-tuple-element.77), channel_id=1, source_target_pairs={{0,8},{8,16},{16,24},{1,9},{9,17},{17,25},{2,10},{10,18},{18,26},{... | collective-permute-start | bytes 196616 | tf_op jit(solution)/shard_map/ppermute | solution.py:24
  160.9 7.4 %collective-permute-start.9 = (bf16[2,32,4,1,128]{1,2,4,3,0:T(4,128)(2,1)}, bf16[2,32,4,1,128]{1,2,4,3,0:T(4,128)(2,1)}, u32[]{:S(2)}, u32[]{:S(2)}) collective-permute-start(bf16[2,32,4,1,128]{1,2,4,3,0:T(4,128)(2,1)} %get-tuple-element.78), channel_id=1, source_target_pairs={{8,0},{16,8},{24,16},{9,1},{17,9},{25,17},{10,2},{18,10},{26,18},{... | collective-permute-start | bytes 196616 | tf_op jit(solution)/shard_map/ppermute | solution.py:27
  176.8 23.2 %collective-permute-start.10 = (bf16[2,32,4,18,1]{1,2,4,3,0:T(4,128)(2,1)S(1)}, bf16[2,32,4,18,1]{1,2,4,3,0:T(4,128)(2,1)S(1)}, u32[]{:S(2)}, u32[]{:S(2)}) collective-permute-start(bf16[2,32,4,18,1]{1,2,4,3,0:T(4,128)(2,1)S(1)} %get-tuple-element.73), channel_id=1, source_target_pairs={{0,1},{1,2},{2,3},{3,4},{4,5},{5,6},{6,7},{8,9},{9,10},{10,11},{11... | collective-permute-start | bytes 27656 | tf_op jit(solution)/shard_map/ppermute | solution.py:24
  178.6 20.5 %collective-permute-start.11 = (bf16[2,32,4,18,1]{1,2,4,3,0:T(4,128)(2,1)S(1)}, bf16[2,32,4,18,1]{1,2,4,3,0:T(4,128)(2,1)S(1)}, u32[]{:S(2)}, u32[]{:S(2)}) collective-permute-start(bf16[2,32,4,18,1]{1,2,4,3,0:T(4,128)(2,1)S(1)} %get-tuple-element.74), channel_id=1, source_target_pairs={{1,0},{2,1},{3,2},{4,3},{5,4},{6,5},{7,6},{9,8},{10,9},{11,10},{12... | collective-permute-start | bytes 27656 | tf_op jit(solution)/shard_map/ppermute | solution.py:27
  253.4 29.2 %copy-start.152 = (f32[32]{0:T(128)S(1)}, f32[32]{0:T(128)}, u32[]{:S(2)}) copy-start(f32[32]{0:T(128)} %param.15) | copy-start | bytes 388
  253.4 29.3 %copy-start.106 = (bf16[32,2,16,128]{3,2,1,0:T(8,128)(2,1)S(1)}, bf16[32,2,16,128]{3,2,1,0:T(8,128)(2,1)}, u32[]{:S(2)}) copy-start(bf16[32,2,16,128]{3,2,1,0:T(8,128)(2,1)} %param.17) | copy-start | bytes 786436
  253.4 29.3 %copy-start.151 = (f32[32]{0:T(128)S(1)}, f32[32]{0:T(128)}, u32[]{:S(2)}) copy-start(f32[32]{0:T(128)} %param.16) | copy-start | bytes 388
  318.2 18.2 %collective-permute-start.12 = (bf16[32,1,16,128]{3,0,2,1:T(8,128)(2,1)}, bf16[32,1,16,128]{3,0,2,1:T(8,128)(2,1)S(1)}, u32[]{:S(2)}, u32[]{:S(2)}) collective-permute-start(bf16[32,1,16,128]{3,0,2,1:T(8,128)(2,1)} %get-tuple-element.269), channel_id=1, source_target_pairs={{0,32},{32,64},{64,96},{1,33},{33,65},{65,97},{2,34},{34,66},{66,9... | collective-permute-start | bytes 393224 | tf_op jit(solution)/shard_map/ppermute | solution.py:24
  327.6 8.8 %collective-permute-start.13 = (bf16[32,1,16,128]{3,0,2,1:T(8,128)(2,1)S(1)}, bf16[32,1,16,128]{3,0,2,1:T(8,128)(2,1)S(1)}, u32[]{:S(2)}, u32[]{:S(2)}) collective-permute-start(bf16[32,1,16,128]{3,0,2,1:T(8,128)(2,1)S(1)} %get-tuple-element.270), channel_id=1, source_target_pairs={{32,0},{64,32},{96,64},{33,1},{65,33},{97,65},{34,2},{66,34},{98,6... | collective-permute-start | bytes 393224 | tf_op jit(solution)/shard_map/ppermute | solution.py:27
  336.4 6.3 %collective-permute-start.14 = (bf16[32,4,1,128]{3,0,2,1:T(8,128)(2,1)S(1)}, bf16[32,4,1,128]{3,0,2,1:T(8,128)(2,1)S(1)}, u32[]{:S(2)}, u32[]{:S(2)}) collective-permute-start(bf16[32,4,1,128]{3,0,2,1:T(8,128)(2,1)S(1)} %get-tuple-element.255), channel_id=1, source_target_pairs={{0,8},{8,16},{16,24},{1,9},{9,17},{17,25},{2,10},{10,18},{18,26},{... | collective-permute-start | bytes 98312 | tf_op jit(solution)/shard_map/ppermute | solution.py:24
  339.8 4.7 collective-permute-start.15
  346.7 7.0 %collective-permute-start.17 = (bf16[32,4,18,1]{0,2,3,1:T(8,128)(2,1)S(1)}, bf16[32,4,18,1]{0,2,3,1:T(8,128)(2,1)}, u32[]{:S(2)}, u32[]{:S(2)}) collective-permute-start(bf16[32,4,18,1]{0,2,3,1:T(8,128)(2,1)S(1)} %copy.531), channel_id=1, source_target_pairs={{1,0},{2,1},{3,2},{4,3},{5,4},{6,5},{7,6},{9,8},{10,9},{11,10},{12... | collective-permute-start | bytes 13832 | tf_op jit(solution)/shard_map/ppermute | solution.py:27
  348.0 5.1 collective-permute-start.16
  366.1 31.5 %copy-start.22 = (f32[4,8,32,128]{3,2,1,0:T(8,128)S(1)}, f32[4,8,32,128]{3,2,1,0:T(8,128)}, u32[]{:S(2)}) copy-start(f32[4,8,32,128]{3,2,1,0:T(8,128)} %copy-done.21) | copy-start | bytes 1572868
  398.3 19.1 %collective-permute-start.18 = (bf16[32,1,16,128]{3,0,2,1:T(8,128)(2,1)S(1)}, bf16[32,1,16,128]{3,0,2,1:T(8,128)(2,1)S(1)}, u32[]{:S(2)}, u32[]{:S(2)}) collective-permute-start(bf16[32,1,16,128]{3,0,2,1:T(8,128)(2,1)S(1)} %get-tuple-element.264), channel_id=1, source_target_pairs={{0,32},{32,64},{64,96},{1,33},{33,65},{65,97},{2,34},{34,66},{66,9... | collective-permute-start | bytes 393224 | tf_op jit(solution)/shard_map/ppermute | solution.py:24
  408.7 8.7 %collective-permute-start.19 = (bf16[32,1,16,128]{3,0,2,1:T(8,128)(2,1)S(1)}, bf16[32,1,16,128]{3,0,2,1:T(8,128)(2,1)S(1)}, u32[]{:S(2)}, u32[]{:S(2)}) collective-permute-start(bf16[32,1,16,128]{3,0,2,1:T(8,128)(2,1)S(1)} %get-tuple-element.265), channel_id=1, source_target_pairs={{32,0},{64,32},{96,64},{33,1},{65,33},{97,65},{34,2},{66,34},{98,6... | collective-permute-start | bytes 393224 | tf_op jit(solution)/shard_map/ppermute | solution.py:27
  417.4 5.5 collective-permute-start.20
  421.1 4.7 collective-permute-start.21
  427.4 6.8 %collective-permute-start.23 = (bf16[32,4,18,1]{0,2,3,1:T(8,128)(2,1)S(1)}, bf16[32,4,18,1]{0,2,3,1:T(8,128)(2,1)S(1)}, u32[]{:S(2)}, u32[]{:S(2)}) collective-permute-start(bf16[32,4,18,1]{0,2,3,1:T(8,128)(2,1)S(1)} %copy.546), channel_id=1, source_target_pairs={{1,0},{2,1},{3,2},{4,3},{5,4},{6,5},{7,6},{9,8},{10,9},{11,10},{12... | collective-permute-start | bytes 13832 | tf_op jit(solution)/shard_map/ppermute | solution.py:27
  428.7 4.9 collective-permute-start.22
  (146 other events, 483.7 us)
Sparse Core Ops, SparseCore 0:
  417.5 145.4 all-reduce.22
where the time goes:
time: 580 us; the launch traced here: 574 us
  waiting for transfers between devices  142 us (24%)
  local copies, waits for them, and re-layouts  139 us (24%)
  blocking collectives  119 us (21%)
  starting transfers between devices  80.6 us (14%)
  other arithmetic  40.1 us (7%)
  matrix products  36.2 us (6%)
  between operations  17.5 us (3%)
    psum x20, blocking collectives, by_axis(): return functools.reduce(lax.psum, axes, value)  119 us
    psum x1, waiting for transfers between devices, body(): grad_w_first = lax.psum(local_first, GX_GY_GZ)  118 us
    ppermute x12, starting transfers between devices, extended(): lax.ppermute(lax.slice_in_dim(block, block.shape[dim] - width, None, axis...  62 us
    dot_general x18, local copies, waits for them, and re-layouts, kernel_grad(): lax.dot_general(flat, stacked, (((1,), (1,)), ((), ())), preferred_elemen...  25.1 us
    dot_general x54, matrix products, convolve(): total = total + jnp.dot(matrix, stacked, preferred_element_type=jnp.float32)  24.7 us
    unnamed x315, local copies, waits for them, and re-layouts  23.5 us
    concatenate x4, local copies, waits for them, and re-layouts, extended(): block = jnp.concatenate([low, block, high], axis=dim)  22.8 us
    concatenate x12, other arithmetic, extended(): block = jnp.concatenate([low, block, high], axis=dim)  21.5 us
  transfers between devices with their start and end apart: 25, of which 12 were waited for; matrix products, arithmetic and copies ran while one was open for 12% of the time, Pallas kernels for 0%

commit v1 on v0

--- a/solution.py
+++ b/solution.py
@@ -10,6 +10,12 @@
 GX = ("gx_0", "gx_1")
 GZ = ("gz_0", "gz_1")
 EPSILON = 1e-05
+
+
+def add_all(x, mesh_axis):
+    shards = lax.all_gather(x, mesh_axis, axis=0, tiled=False)
+    result = shards.sum(axis=0)
+    return result
 
 
 def by_axis(value, axes):
@@ -155,7 +161,7 @@
     local_first = kernel_grad(input_pad_b, delta_one) * factor
     delta_pad_one = extended(delta_one, ((GX, 1), ("gy", 2), (GZ, 3)), 1)
     dx_b = convolve(delta_pad_one, flipped(w_first)).astype(jnp.bfloat16)
-    grad_w_first = lax.psum(local_first, GX_GY_GZ)
+    grad_w_first = add_all(local_first, GX_GY_GZ)
     grad_norm = jnp.stack([sum_x1, sum_d1, sum_x2, sum_d2]) * factor
     return (y_a, dx_b, grad_w_first, grad_w_second, grad_norm)
 

time: 580 us -> 925 us (1.59)
  waiting for transfers between devices: 142 us -> 484 us
  other arithmetic: 40.1 us -> 62 us
    all_gather x0 -> x1, waiting for transfers between devices: none -> 309 us  [add_all(): shards = lax.all_gather(x, mesh_axis, axis=0, tiled=False)]
    reduce_sum x0 -> x1, other arithmetic: none -> 18.9 us  [add_all(): result = shards.sum(axis=0)]
    ppermute x12, waiting for transfers between devices: 20.6 us -> 38 us  [extended(): lax.ppermute(lax.slice_in_dim(block, 0, width, axis=dim), axis, backward)]
    psum x1, waiting for transfers between devices: 118 us -> 130 us  [body(): grad_w_second = lax.psum(local_second, GX_GY_GZ)]
    unnamed x315 -> x306, local copies, waits for them, and re-layouts: 23.5 us -> 29.9 us
  transfers between devices with their start and end apart: 25 -> 26, of which waited for: 12 -> 16; matrix products, arithmetic and copies ran while one was open for 12% -> 10% of each run, Pallas kernels for 0% -> 0%
where the time goes in v1:
time: 925 us; the launch traced here: 919 us
  waiting for transfers between devices  484 us (52%)
  local copies, waits for them, and re-layouts  131 us (14%)
  blocking collectives  114 us (12%)
  starting transfers between devices  74.1 us (8%)
  other arithmetic  62 us (7%)
  matrix products  36.6 us (4%)
  between operations  17.4 us (2%)
    all_gather x1, waiting for transfers between devices, add_all(): shards = lax.all_gather(x, mesh_axis, axis=0, tiled=False)  309 us
    psum x1, waiting for transfers between devices, body(): grad_w_second = lax.psum(local_second, GX_GY_GZ)  130 us
    psum x20, blocking collectives, by_axis(): return functools.reduce(lax.psum, axes, value)  114 us
    ppermute x12, starting transfers between devices, extended(): lax.ppermute(lax.slice_in_dim(block, block.shape[dim] - width, None, axis...  55.4 us
    ppermute x12, waiting for transfers between devices, extended(): lax.ppermute(lax.slice_in_dim(block, 0, width, axis=dim), axis, backward)  38 us
    unnamed x306, local copies, waits for them, and re-layouts  29.9 us
    dot_general x54, matrix products, convolve(): total = total + jnp.dot(matrix, stacked, preferred_element_type=jnp.float32)  25 us
    concatenate x4, local copies, waits for them, and re-layouts, extended(): block = jnp.concatenate([low, block, high], axis=dim)  23.1 us
  transfers between devices with their start and end apart: 26, of which 16 were waited for; matrix products, arithmetic and copies ran while one was open for 10% of the time, Pallas kernels for 0%

profile of v1, /device:TPU:1, one launch (start us, length us, event | category | flops | bytes accessed | tf_op | source)
XLA Modules:
  0.0 918.8 jit_solution(8349542820634315366)
XLA Ops:
  8.4 6.9 collective-permute-start
  18.6 5.9 collective-permute-done.1
  37.0 4.0 collective-permute-done.3
  41.0 6.2 pad_maximum_fusion
  58.6 6.3 copy.464
  98.3 5.3 all-reduce.19
  106.0 7.2 all-reduce.7
  113.2 11.0 %all-reduce.3 = (f32[2,32]{1,0:T(2,128)S(1)}, f32[2,32]{1,0:T(2,128)S(1)}) all-reduce(f32[2,32]{1,0:T(2,128)S(1)} %get-tuple-element.43, f32[2,32]{1,0:T(2,128)S(1)} %get-tuple-element.44), channel_id=1, replica_groups=mesh['gx_0'=2,'gx_1'=2,'gy'=4,'gz_0'=4,'gz_1'=2] {'gz_0'}, use_global_device_ids=true, to_apply=%region_12.0 | all-reduce | flops 128 | bytes 1024 | tf_op jit(solution)/shard_map/psum | solution.py:22
  131.2 10.1 %collective-permute-start.6 = (bf16[2,32,1,16,128]{4,3,2,1,0:T(8,128)(2,1)S(1)}, bf16[2,32,1,16,128]{4,3,2,1,0:T(8,128)(2,1)S(1)}, u32[]{:S(2)}, u32[]{:S(2)}) collective-permute-start(bf16[2,32,1,16,128]{4,3,2,1,0:T(8,128)(2,1)S(1)} %get-tuple-element.255), channel_id=1, source_target_pairs={{0,32},{32,64},{64,96},{1,33},{33,65},{65,97},{2,34},{34,66},{66,9... | collective-permute-start | bytes 786440 | tf_op jit(solution)/shard_map/ppermute | solution.py:30
  144.6 5.9 collective-permute-done.7
  151.6 5.6 copy.493
  167.8 6.2 pad_maximum_fusion.1
  181.6 7.4 copy.497
  230.2 5.3 all-reduce.18
  237.9 6.0 all-reduce.6
  243.9 8.0 all-reduce.2
  260.5 5.3 all-reduce.17
  265.8 8.6 all-reduce.13
  274.4 7.4 all-reduce.5
  281.8 6.2 all-reduce.1
  288.0 4.0 all-reduce.9
  294.1 10.3 %collective-permute-start.12 = (bf16[32,1,16,128]{3,0,2,1:T(8,128)(2,1)S(1)}, bf16[32,1,16,128]{3,0,2,1:T(8,128)(2,1)S(1)}, u32[]{:S(2)}, u32[]{:S(2)}) collective-permute-start(bf16[32,1,16,128]{3,0,2,1:T(8,128)(2,1)S(1)} %get-tuple-element.267), channel_id=1, source_target_pairs={{0,32},{32,64},{64,96},{1,33},{33,65},{65,97},{2,34},{34,66},{66,9... | collective-permute-start | bytes 393224 | tf_op jit(solution)/shard_map/ppermute | solution.py:30
  307.9 4.3 collective-permute-done.13
  352.3 5.4 all-reduce.16
  360.2 8.2 all-reduce.4
  368.4 7.1 all-reduce
  375.5 4.2 all-reduce.8
  406.4 9.2 %collective-permute-start.18 = (bf16[32,1,16,128]{3,0,2,1:T(8,128)(2,1)S(1)}, bf16[32,1,16,128]{3,0,2,1:T(8,128)(2,1)S(1)}, u32[]{:S(2)}, u32[]{:S(2)}) collective-permute-start(bf16[32,1,16,128]{3,0,2,1:T(8,128)(2,1)S(1)} %get-tuple-element.262), channel_id=1, source_target_pairs={{0,32},{32,64},{64,96},{1,33},{33,65},{65,97},{2,34},{34,66},{66,9... | collective-permute-start | bytes 393224 | tf_op jit(solution)/shard_map/ppermute | solution.py:30
  418.9 5.9 collective-permute-done.19
  452.2 308.9 %all-gather.2.cloned.1.call-done = f32[128,3,3,3,32,32]{5,4,3,2,1,0:T(8,128)} async-done(((f32[1,3,3,3,32,32]{5,4,3,2,1,0:T(8,128)}), f32[128,3,3,3,32,32]{5,4,3,2,1,0:T(8,128)}) %all-gather.2.cloned.1.call-update) | async-done | bytes 14155792 | tf_op jit(solution)/shard_map/all_gather | solution.py:16
  761.1 18.9 %reduce_sum.129 = f32[3,3,3,32,32]{4,3,2,1,0:T(8,128)} reduce(f32[128,3,3,3,32,32]{5,4,3,2,1,0:T(8,128)} %all-gather.2.cloned.1.call-done, f32[]{:T(128)} %constant.15.clone.1), dimensions={0}, to_apply=%region_52.53 | reduce | flops 3511296 | bytes 14266372 | tf_op jit(solution)/shard_map/reduce_sum | solution.py:17
  780.0 130.0 %all-reduce.22.cloned.1.call-done = f32[3,3,3,32,32]{4,3,2,1,0:T(8,128)} async-done(((f32[3,3,3,32,32]{4,3,2,1,0:T(8,128)}), f32[3,3,3,32,32]{4,3,2,1,0:T(8,128)}) %all-reduce.22.cloned.1.call-update) | async-done | bytes 110608 | tf_op jit(solution)/shard_map/psum | solution.py:155
  (666 shorter events, 250.7 us)
Async XLA Ops:
  7.2 754.0 %all-gather.2.cloned.1.call-start = ((), (), s32[]{:S(2)}) async-start(), calls=%async_computation | async-start | bytes 57065472 | tf_op jit(solution)/shard_map/all_gather | solution.py:16
  8.4 10.2 %collective-permute-start = (bf16[2,32,1,16,128]{4,3,2,1,0:T(8,128)(2,1)S(1)}, bf16[2,32,1,16,128]{4,3,2,1,0:T(8,128)(2,1)S(1)}, u32[]{:S(2)}, u32[]{:S(2)}) collective-permute-start(bf16[2,32,1,16,128]{4,3,2,1,0:T(8,128)(2,1)S(1)} %get-tuple-element.257), channel_id=1, source_target_pairs={{0,32},{32,64},{64,96},{1,33},{33,65},{65,97},{2,34},{34,66},{66,9... | collective-permute-start | bytes 786440 | tf_op jit(solution)/shard_map/ppermute | solution.py:30
  15.3 9.2 %collective-permute-start.1 = (bf16[2,32,1,16,128]{4,3,2,1,0:T(8,128)(2,1)S(1)}, bf16[2,32,1,16,128]{4,3,2,1,0:T(8,128)(2,1)S(1)}, u32[]{:S(2)}, u32[]{:S(2)}) collective-permute-start(bf16[2,32,1,16,128]{4,3,2,1,0:T(8,128)(2,1)S(1)} %get-tuple-element.258), channel_id=1, source_target_pairs={{32,0},{64,32},{96,64},{33,1},{65,33},{97,65},{34,2},{66,34},{98,6... | collective-permute-start | bytes 786440 | tf_op jit(solution)/shard_map/ppermute | solution.py:33
  30.6 6.4 collective-permute-start.2
  33.7 7.2 collective-permute-start.3
  49.4 15.5 %collective-permute-start.4 = (bf16[2,32,4,18,1]{1,2,4,3,0:T(4,128)(2,1)S(1)}, bf16[2,32,4,18,1]{1,2,4,3,0:T(4,128)(2,1)S(1)}, u32[]{:S(2)}, u32[]{:S(2)}) collective-permute-start(bf16[2,32,4,18,1]{1,2,4,3,0:T(4,128)(2,1)S(1)} %get-tuple-element.73), channel_id=1, source_target_pairs={{0,1},{1,2},{2,3},{3,4},{4,5},{5,6},{6,7},{8,9},{9,10},{10,11},{11... | collective-permute-start | bytes 27656 | tf_op jit(solution)/shard_map/ppermute | solution.py:30
  52.0 13.8 %collective-permute-start.5 = (bf16[2,32,4,18,1]{1,2,4,3,0:T(4,128)(2,1)S(1)}, bf16[2,32,4,18,1]{1,2,4,3,0:T(4,128)(2,1)}, u32[]{:S(2)}, u32[]{:S(2)}) collective-permute-start(bf16[2,32,4,18,1]{1,2,4,3,0:T(4,128)(2,1)S(1)} %get-tuple-element.74), channel_id=1, source_target_pairs={{1,0},{2,1},{3,2},{4,3},{5,4},{6,5},{7,6},{9,8},{10,9},{11,10},{12... | collective-permute-start | bytes 27656 | tf_op jit(solution)/shard_map/ppermute | solution.py:33
  95.7 33.9 %copy-start.127 = (f32[32]{0:T(128)S(1)}, f32[32]{0:T(128)}, u32[]{:S(2)}) copy-start(f32[32]{0:T(128)} %param.14) | copy-start | bytes 388
  95.7 33.9 %copy-start.130 = (f32[32]{0:T(128)S(1)}, f32[32]{0:T(128)}, u32[]{:S(2)}) copy-start(f32[32]{0:T(128)} %param.13) | copy-start | bytes 388
  131.2 13.4 %collective-permute-start.6 = (bf16[2,32,1,16,128]{4,3,2,1,0:T(8,128)(2,1)S(1)}, bf16[2,32,1,16,128]{4,3,2,1,0:T(8,128)(2,1)S(1)}, u32[]{:S(2)}, u32[]{:S(2)}) collective-permute-start(bf16[2,32,1,16,128]{4,3,2,1,0:T(8,128)(2,1)S(1)} %get-tuple-element.255), channel_id=1, source_target_pairs={{0,32},{32,64},{64,96},{1,33},{33,65},{65,97},{2,34},{34,66},{66,9... | collective-permute-start | bytes 786440 | tf_op jit(solution)/shard_map/ppermute | solution.py:30
  141.3 9.2 %collective-permute-start.7 = (bf16[2,32,1,16,128]{4,3,2,1,0:T(8,128)(2,1)S(1)}, bf16[2,32,1,16,128]{4,3,2,1,0:T(8,128)(2,1)S(1)}, u32[]{:S(2)}, u32[]{:S(2)}) collective-permute-start(bf16[2,32,1,16,128]{4,3,2,1,0:T(8,128)(2,1)S(1)} %get-tuple-element.256), channel_id=1, source_target_pairs={{32,0},{64,32},{96,64},{33,1},{65,33},{97,65},{34,2},{66,34},{98,6... | collective-permute-start | bytes 786440 | tf_op jit(solution)/shard_map/ppermute | solution.py:33
  158.5 5.5 collective-permute-start.8
  160.7 7.1 collective-permute-start.9
  176.2 12.8 %collective-permute-start.10 = (bf16[2,32,4,18,1]{1,2,4,3,0:T(4,128)(2,1)S(1)}, bf16[2,32,4,18,1]{1,2,4,3,0:T(4,128)(2,1)S(1)}, u32[]{:S(2)}, u32[]{:S(2)}) collective-permute-start(bf16[2,32,4,18,1]{1,2,4,3,0:T(4,128)(2,1)S(1)} %get-tuple-element.71), channel_id=1, source_target_pairs={{0,1},{1,2},{2,3},{3,4},{4,5},{5,6},{6,7},{8,9},{9,10},{10,11},{11... | collective-permute-start | bytes 27656 | tf_op jit(solution)/shard_map/ppermute | solution.py:30
  178.6 12.4 %collective-permute-start.11 = (bf16[2,32,4,18,1]{1,2,4,3,0:T(4,128)(2,1)S(1)}, bf16[2,32,4,18,1]{1,2,4,3,0:T(4,128)(2,1)S(1)}, u32[]{:S(2)}, u32[]{:S(2)}) collective-permute-start(bf16[2,32,4,18,1]{1,2,4,3,0:T(4,128)(2,1)S(1)} %get-tuple-element.72), channel_id=1, source_target_pairs={{1,0},{2,1},{3,2},{4,3},{5,4},{6,5},{7,6},{9,8},{10,9},{11,10},{12... | collective-permute-start | bytes 27656 | tf_op jit(solution)/shard_map/ppermute | solution.py:33
  227.6 30.0 %copy-start.102 = (bf16[32,2,16,128]{3,2,1,0:T(8,128)(2,1)S(1)}, bf16[32,2,16,128]{3,2,1,0:T(8,128)(2,1)}, u32[]{:S(2)}) copy-start(bf16[32,2,16,128]{3,2,1,0:T(8,128)(2,1)} %param.17) | copy-start | bytes 786436
  227.6 30.0 %copy-start.147 = (f32[32]{0:T(128)S(1)}, f32[32]{0:T(128)}, u32[]{:S(2)}) copy-start(f32[32]{0:T(128)} %param.16) | copy-start | bytes 388
  260.5 55.6 %copy-start.126 = (f32[2,32]{1,0:T(2,128)S(1)}, f32[2,32]{1,0:T(2,128)}, u32[]{:S(2)}) copy-start(f32[2,32]{1,0:T(2,128)} %copy-done.125) | copy-start | bytes 772
  260.5 55.7 %copy-start.131 = (f32[32]{0:T(128)S(1)}, f32[32]{0:T(128)}, u32[]{:S(2)}) copy-start(f32[32]{0:T(128)} %param.13) | copy-start | bytes 388
  294.1 13.8 %collective-permute-start.12 = (bf16[32,1,16,128]{3,0,2,1:T(8,128)(2,1)S(1)}, bf16[32,1,16,128]{3,0,2,1:T(8,128)(2,1)S(1)}, u32[]{:S(2)}, u32[]{:S(2)}) collective-permute-start(bf16[32,1,16,128]{3,0,2,1:T(8,128)(2,1)S(1)} %get-tuple-element.267), channel_id=1, source_target_pairs={{0,32},{32,64},{64,96},{1,33},{33,65},{65,97},{2,34},{34,66},{66,9... | collective-permute-start | bytes 393224 | tf_op jit(solution)/shard_map/ppermute | solution.py:30
  304.4 7.8 collective-permute-start.13
  312.8 15.0 %collective-permute-start.14 = (bf16[32,4,1,128]{3,0,2,1:T(8,128)(2,1)}, bf16[32,4,1,128]{3,0,2,1:T(8,128)(2,1)S(1)}, u32[]{:S(2)}, u32[]{:S(2)}) collective-permute-start(bf16[32,4,1,128]{3,0,2,1:T(8,128)(2,1)} %get-tuple-element.253), channel_id=1, source_target_pairs={{0,8},{8,16},{16,24},{1,9},{9,17},{17,25},{2,10},{10,18},{18,26},{... | collective-permute-start | bytes 98312 | tf_op jit(solution)/shard_map/ppermute | solution.py:30
  314.6 13.2 %collective-permute-start.15 = (bf16[32,4,1,128]{3,0,2,1:T(8,128)(2,1)}, bf16[32,4,1,128]{3,0,2,1:T(8,128)(2,1)S(1)}, u32[]{:S(2)}, u32[]{:S(2)}) collective-permute-start(bf16[32,4,1,128]{3,0,2,1:T(8,128)(2,1)} %get-tuple-element.254), channel_id=1, source_target_pairs={{8,0},{16,8},{24,16},{9,1},{17,9},{25,17},{10,2},{18,10},{26,18},{... | collective-permute-start | bytes 98312 | tf_op jit(solution)/shard_map/ppermute | solution.py:33
  329.9 6.0 collective-permute-start.16
  333.6 4.6 collective-permute-start.17
  386.9 523.1 %all-reduce.22.cloned.1.call-start = ((), (), s32[]{:S(2)}) async-start(), calls=%async_computation.1 | async-start | bytes 884736 | tf_op jit(solution)/shard_map/psum | solution.py:155
  406.4 12.5 %collective-permute-start.18 = (bf16[32,1,16,128]{3,0,2,1:T(8,128)(2,1)S(1)}, bf16[32,1,16,128]{3,0,2,1:T(8,128)(2,1)S(1)}, u32[]{:S(2)}, u32[]{:S(2)}) collective-permute-start(bf16[32,1,16,128]{3,0,2,1:T(8,128)(2,1)S(1)} %get-tuple-element.262), channel_id=1, source_target_pairs={{0,32},{32,64},{64,96},{1,33},{33,65},{65,97},{2,34},{34,66},{66,9... | collective-permute-start | bytes 393224 | tf_op jit(solution)/shard_map/ppermute | solution.py:30
  415.7 9.2 collective-permute-start.19
  424.8 3.2 collective-permute-start.20
  426.1 5.3 collective-permute-start.21
  432.6 4.7 collective-permute-start.22
  435.8 5.2 collective-permute-start.23
  (143 other events, 474.3 us)
Sparse Core Ops, SparseCore 0:
  387.0 374.0 all-gather.1
  765.9 144.0 all-reduce.21
